TPU v7x, 8 devices: a whole 2x2x1 slice. The times are simulated.
8 devices in a mesh: pp: 4 (over z, y, x), dp: 2 (over core).
Axes of the slice: x: 2, y: 2, z: 1, core: 2. Of those that a mesh axis runs over, the one named last changes fastest.
Arguments:
- tok_ids: int32 [4, 1024], P(None, 'dp')
- d_out: bfloat16 [4, 1024, 128], P('pp', 'dp')
- stored_x: bfloat16 [4, 4, 1024, 128], P('pp', None, 'dp')
- w_in: bfloat16 [32, 128, 512], P('pp')
- w_out: bfloat16 [32, 512, 128], P('pp')
- acc_in: float32 [32, 2, 128, 512], P('pp', 'dp')
- acc_out: float32 [32, 2, 512, 128], P('pp', 'dp')
- acc_emb: float32 [2, 30522, 128], P('dp')
Outputs:
- output 1: float32 [32, 128, 512], P('pp', 'dp')
- output 2: float32 [32, 512, 128], P('pp', 'dp')
- output 3: float32 [30522, 128], P(None, 'dp')
All inputs are finite; a program needn't handle non-finite values.
Results may differ from a plain program's by a relative error of at most 0.016148.
Values are sent between devices in bfloat16 or wider.
A program may use at most 1 GiB of HBM per device.

v0:
```python
import functools

import jax
import jax.numpy as jnp
from jax import lax
from jax.experimental import pallas as pl
from jax.experimental.pallas import tpu as pltpu
from jax.sharding import PartitionSpec as P

MESH = pl.DeviceIdType.MESH
F32 = jnp.float32
BF16 = jnp.bfloat16
NT = (((1,), (1,)), ((), ()))
C0 = 0.7978845608028654
C1 = 0.7978845608028654 * 0.044715
FF_CHUNK = 256
VOCAB_BLOCK = 2048
VOCAB_TILE = 256


def gelu_parts(pre_act):
    square = pre_act * pre_act
    tanh_val = jnp.tanh(pre_act * (C0 + C1 * square))
    half = 0.5 + 0.5 * tanh_val
    value = pre_act * half
    slope = half + (value - value * half) * (2.0 * C0 + (6.0 * C1) * square)
    return value, slope


def forward_layer(layer_id, w_in, w_out, acts_x, acts_a, acts_s):
    x_cur = acts_x[layer_id]
    out_x = x_cur.astype(F32)
    for start in range(0, w_in.shape[2], FF_CHUNK):
        cols = pl.ds(start, FF_CHUNK)
        pre_act = jnp.dot(x_cur, w_in[layer_id, :, cols], preferred_element_type=F32).astype(BF16)
        value, slope = gelu_parts(pre_act.astype(F32))
        hidden = value.astype(BF16)
        acts_a[layer_id, :, cols] = hidden
        acts_s[layer_id, :, cols] = slope
        out_x += jnp.dot(hidden, w_out[layer_id, cols, :], preferred_element_type=F32)
    acts_x[layer_id + 1] = out_x.astype(BF16)


def backward_layer(layer_id, w_in, w_out, acts_x, acts_a, acts_s, cot, sum_in, sum_out_t):
    cot_cur = cot[...]
    cot_t = cot_cur.T
    x_t = acts_x[layer_id].T
    d_x = cot_cur.astype(F32)
    for start in range(0, w_in.shape[2], FF_CHUNK):
        cols = pl.ds(start, FF_CHUNK)
        d_hidden = lax.dot_general(cot_cur, w_out[layer_id, cols, :], NT, preferred_element_type=F32).astype(BF16)
        d_pre = (d_hidden.astype(F32) * acts_s[layer_id, :, cols]).astype(BF16)
        d_x += lax.dot_general(d_pre, w_in[layer_id, :, cols], NT, preferred_element_type=F32)
        sum_out_t[layer_id, :, cols] += jnp.dot(cot_t, acts_a[layer_id, :, cols], preferred_element_type=F32)
        sum_in[layer_id, :, cols] += jnp.dot(x_t, d_pre, preferred_element_type=F32)
    cot[...] = d_x.astype(BF16)


def stage_kernel(stages, ids, d_out, stored_x, w_in, w_out, acc_in, acc_out, acc_emb,
                 ids_peer, acc_peer, dx_all, gi_own, gi_recv, go_own, go_recv,
                 acts_x, acts_a, acts_s, cot, dx_send, cot_in, sum_in, sum_out_t, acc_o, gi_bf, go_bf,
                 load_sem, ex_send, ex_recv, cot_send, cot_recv, bc_send, bc_recv, pr_send, pr_recv, loc_sem, g_sem, g_send, g_recv):
    stage = lax.axis_index('pp')
    rep = lax.axis_index('dp')
    other = 1 - rep
    layers = w_in.shape[0]
    last = stages - 1

    barrier = pltpu.get_barrier_semaphore()
    for hop in range(1, 2 * stages):
        place = lax.rem(stage * 2 + rep + hop, 2 * stages)
        pl.semaphore_signal(barrier, inc=1, device_id=(place // 2, lax.rem(place, 2)), device_id_type=MESH)

    load_in = pltpu.make_async_copy(acc_in, sum_in, load_sem.at[0])
    load_out = pltpu.make_async_copy(acc_out, acc_o, load_sem.at[1])
    load_in.start()
    load_out.start()
    sum_out_t[...] = jnp.zeros_like(sum_out_t)

    def forward(step_id):
        acts_x[0] = stored_x[last - stage - step_id]
        pl.loop(0, layers)(lambda layer_id: forward_layer(layer_id, w_in, w_out, acts_x, acts_a, acts_s))

    forward(0)
    pl.semaphore_wait(barrier, 2 * stages - 1)

    ex_ids = pltpu.make_async_remote_copy(ids, ids_peer, ex_send.at[0], ex_recv.at[0], device_id=(stage, other), device_id_type=MESH)
    ex_emb = pltpu.make_async_remote_copy(acc_emb, acc_peer, ex_send.at[1], ex_recv.at[1], device_id=(stage, other), device_id_type=MESH)
    ex_ids.start()
    ex_emb.start()
    load_in.wait()
    load_out.wait()

    def cot_copy(step_id):
        return pltpu.make_async_remote_copy(dx_send.at[step_id], cot_in.at[step_id], cot_send.at[step_id], cot_recv.at[step_id],
                                            device_id=(jnp.maximum(stage - 1, 0), rep), device_id_type=MESH)

    def bc_copy(step_id, target):
        return pltpu.make_async_remote_copy(dx_send.at[step_id], dx_all.at[rep, last - step_id], bc_send.at[target, step_id], bc_recv.at[step_id],
                                            device_id=(target, rep), device_id_type=MESH)

    def peer_copy(step_id, src):
        return pltpu.make_async_remote_copy(src, dx_all.at[rep, last - step_id], pr_send.at[step_id], pr_recv.at[step_id],
                                            device_id=(stage, other), device_id_type=MESH)

    def local_copy(step_id):
        return pltpu.make_async_copy(dx_send.at[step_id], dx_all.at[rep, last - step_id], loc_sem.at[step_id])

    @pl.loop(0, stages)
    def _(step_id):
        @pl.when(stage + step_id <= last)
        def _():
            @pl.when(step_id == 0)
            def _():
                cot[...] = d_out[...]

            @pl.when(step_id > 0)
            def _():
                forward(step_id)
                cot_copy(step_id - 1).wait_recv()
                cot[...] = cot_in[step_id - 1]

            pl.loop(0, layers)(lambda back_id: backward_layer(layers - 1 - back_id, w_in, w_out, acts_x, acts_a, acts_s, cot, sum_in, sum_out_t))
            dx_send[step_id] = cot[...]

            @pl.when(stage > 0)
            def _():
                cot_copy(step_id).start()

            @pl.when(stage == 0)
            def _():
                for target in range(1, stages):
                    bc_copy(step_id, target).start()
                peer_copy(step_id, dx_send.at[step_id]).start()
                local_copy(step_id).start()

    @pl.loop(0, layers)
    def _(layer_id):
        gi_bf[layer_id] = sum_in[layer_id].astype(BF16)
        go_bf[layer_id] = (sum_out_t[layer_id].T + acc_o[layer_id]).astype(BF16)

    half_i = gi_own.shape[1]
    half_o = go_own.shape[1]
    keep = [
        pltpu.make_async_copy(gi_bf.at[:, pl.ds(pl.multiple_of(rep * half_i, half_i), half_i), :], gi_own, g_sem.at[0]),
        pltpu.make_async_copy(go_bf.at[:, pl.ds(pl.multiple_of(rep * half_o, half_o), half_o), :], go_own, g_sem.at[1]),
    ]
    give = [
        pltpu.make_async_remote_copy(gi_bf.at[:, pl.ds(pl.multiple_of(other * half_i, half_i), half_i), :], gi_recv, g_send.at[0], g_recv.at[0], device_id=(stage, other), device_id_type=MESH),
        pltpu.make_async_remote_copy(go_bf.at[:, pl.ds(pl.multiple_of(other * half_o, half_o), half_o), :], go_recv, g_send.at[1], g_recv.at[1], device_id=(stage, other), device_id_type=MESH),
    ]
    for copy in keep + give:
        copy.start()

    @pl.when(stage > 0)
    def _():
        for step_id in range(stages):
            bc_copy(step_id, 0).wait_recv()
            peer_copy(step_id, dx_all.at[rep, last - step_id]).start()
        for step_id in range(stages):
            @pl.when(stage + step_id <= last)
            def _():
                cot_copy(step_id).wait_send()

    @pl.when(stage == 0)
    def _():
        for step_id in range(stages):
            for target in range(1, stages):
                bc_copy(step_id, target).wait_send()
            local_copy(step_id).wait()

    for step_id in range(stages):
        peer_copy(step_id, dx_send.at[step_id]).wait()
    for copy in keep + give:
        copy.wait()
    ex_ids.wait()
    ex_emb.wait()


def finish_kernel(vocab, ids_own, ids_peer, acc_own, acc_peer, dx_all, gi_own, gi_recv, go_own, go_recv,
                  emb_t, grad_in, grad_out, tab_own, tab_peer, dxf, sems):
    step = pl.program_id(0)
    rep = lax.axis_index('dp')
    padded = tab_own.shape[0]
    rows_own = tab_own.reshape(padded, tab_own.shape[2])
    rows_peer = tab_peer.reshape(padded, tab_peer.shape[2])
    micros, tokens = ids_own.shape

    @pl.when(step == 0)
    def _():
        load_own = pltpu.make_async_copy(acc_own, tab_own.at[pl.ds(0, vocab)], sems.at[0])
        load_peer = pltpu.make_async_copy(acc_peer, tab_peer.at[pl.ds(0, vocab)], sems.at[1])
        load_own.start()
        load_peer.start()
        grad_in[...] = (gi_own[...].astype(F32) + gi_recv[...].astype(F32)) * 0.5
        grad_out[...] = (go_own[...].astype(F32) + go_recv[...].astype(F32)) * 0.5
        dxf[0] = dx_all[rep].astype(F32)
        dxf[1] = dx_all[1 - rep].astype(F32)
        load_own.wait()
        load_peer.wait()
        for micro in range(micros):
            def add_rows(row, carry):
                first = ids_own[micro, row]
                second = ids_peer[micro, row]
                rows_own[pl.ds(first, 1), :] = rows_own[pl.ds(first, 1), :] + dxf[0, micro, pl.ds(row, 1), :]
                rows_peer[pl.ds(second, 1), :] = rows_peer[pl.ds(second, 1), :] + dxf[1, micro, pl.ds(row, 1), :]
                return carry
            lax.fori_loop(0, tokens, add_rows, 0, unroll=8)

    half = emb_t.shape[0]
    width = tab_own.shape[2]
    row_id = lax.broadcasted_iota(jnp.int32, (half, 2 * width), 0)
    col_id = lax.broadcasted_iota(jnp.int32, (half, 2 * width), 1)
    pick = jnp.where(lax.rem(col_id, width) == row_id + half * rep, 0.5, 0.0).astype(BF16)
    for start in range(0, emb_t.shape[1], VOCAB_TILE):
        first = pl.multiple_of(step * emb_t.shape[1] + start, 8)
        both = jnp.concatenate([rows_own[pl.ds(first, VOCAB_TILE), :].astype(BF16), rows_peer[pl.ds(first, VOCAB_TILE), :].astype(BF16)], axis=1)
        emb_t[:, start:start + VOCAB_TILE] = lax.dot_general(pick, both, NT, preferred_element_type=F32)


def solution(mesh):
    stages = mesh.shape['pp']

    def device_body(tok_ids, d_out, stored_x, w_in, w_out, acc_in, acc_out, acc_emb):
        layers, hid, ff = w_in.shape
        tokens = d_out.shape[1]
        vocab = acc_emb.shape[1]
        half_i, half_o, half_e = hid // 2, ff // 2, hid // 2
        emb_rows = acc_emb.reshape(vocab, 1, hid)
        any_spec = pl.BlockSpec(memory_space=pl.ANY)
        vmem_spec = pl.BlockSpec(memory_space=pltpu.VMEM)
        dma = pltpu.SemaphoreType.DMA
        ids_peer, acc_peer, dx_all, gi_own, gi_recv, go_own, go_recv = pl.pallas_call(
            functools.partial(stage_kernel, stages),
            name='stage_pipeline',
            in_specs=[any_spec] + [vmem_spec] * 4 + [any_spec] * 3,
            out_specs=[any_spec] * 7,
            out_shape=[
                jax.ShapeDtypeStruct(tok_ids.shape, tok_ids.dtype),
                jax.ShapeDtypeStruct((vocab, 1, hid), F32),
                jax.ShapeDtypeStruct((2, stages, tokens, hid), BF16),
                jax.ShapeDtypeStruct((layers, half_i, ff), BF16),
                jax.ShapeDtypeStruct((layers, half_i, ff), BF16),
                jax.ShapeDtypeStruct((layers, half_o, hid), BF16),
                jax.ShapeDtypeStruct((layers, half_o, hid), BF16),
            ],
            scratch_shapes=[
                pltpu.VMEM((layers + 1, tokens, hid), BF16),
                pltpu.VMEM((layers, tokens, ff), BF16),
                pltpu.VMEM((layers, tokens, ff), F32),
                pltpu.VMEM((tokens, hid), BF16),
                pltpu.VMEM((stages, tokens, hid), BF16),
                pltpu.VMEM((stages, tokens, hid), BF16),
                pltpu.VMEM((layers, hid, ff), F32),
                pltpu.VMEM((layers, hid, ff), F32),
                pltpu.VMEM((layers, ff, hid), F32),
                pltpu.VMEM((layers, hid, ff), BF16),
                pltpu.VMEM((layers, ff, hid), BF16),
                dma((2,)), dma((2,)), dma((2,)),
                dma((stages,)), dma((stages,)),
                dma((stages, stages)), dma((stages,)),
                dma((stages,)), dma((stages,)), dma((stages,)),
                dma((2,)), dma((2,)), dma((2,)),
            ],
            compiler_params=pltpu.CompilerParams(collective_id=0, has_side_effects=True, vmem_limit_bytes=60 * 2**20),
        )(tok_ids, d_out[0], stored_x[0], w_in, w_out, acc_in[:, 0], acc_out[:, 0], emb_rows)

        padded = pl.cdiv(vocab, VOCAB_BLOCK) * VOCAB_BLOCK
        whole = lambda shape: pl.BlockSpec(shape, lambda step: (0,) * len(shape))
        smem_spec = pl.BlockSpec(memory_space=pltpu.SMEM)
        emb_t, grad_in, grad_out = pl.pallas_call(
            functools.partial(finish_kernel, vocab),
            name='finish',
            grid=(pl.cdiv(vocab, VOCAB_BLOCK),),
            in_specs=[smem_spec] * 2 + [any_spec] * 2 + [whole(v.shape) for v in (dx_all, gi_own, gi_recv, go_own, go_recv)],
            out_specs=[pl.BlockSpec((half_e, VOCAB_BLOCK), lambda step: (0, step)), whole((layers, half_i, ff)), whole((layers, half_o, hid))],
            out_shape=[
                jax.ShapeDtypeStruct((half_e, vocab), F32),
                jax.ShapeDtypeStruct((layers, half_i, ff), F32),
                jax.ShapeDtypeStruct((layers, half_o, hid), F32),
            ],
            scratch_shapes=[
                pltpu.VMEM((padded, 1, hid), F32),
                pltpu.VMEM((padded, 1, hid), F32),
                pltpu.VMEM((2, stages, tokens, hid), F32),
                dma((2,)),
            ],
            compiler_params=pltpu.CompilerParams(vmem_limit_bytes=60 * 2**20),
        )(tok_ids, ids_peer, emb_rows, acc_peer, dx_all, gi_own, gi_recv, go_own, go_recv)
        return grad_in, grad_out, emb_t.T

    return jax.shard_map(device_body, mesh=mesh, in_specs=(P(None, 'dp'), P('pp', 'dp', None), P('pp', None, 'dp', None), P('pp', None, None), P('pp', None, None), P('pp', 'dp', None, None), P('pp', 'dp', None, None), P('dp', None, None)), out_specs=(P('pp', 'dp', None), P('pp', 'dp', None), P(None, 'dp')), check_vma=False)
```

profile of v0, /device:TPU:7, one launch (start us, length us, event | category | flops | bytes accessed | tf_op | source)
XLA Modules:
  0.0 92.1 jit_solution(10398007796088443242)
XLA Ops:
  0.6 58.6 %stage_pipeline.1 = (s32[4,512]{1,0:T(4,128)}, f32[30522,1,128]{2,1,0:T(1,128)}, bf16[2,4,512,128]{3,2,1,0:T(8,128)(2,1)}, bf16[8,64,512]{2,1,0:T(8,128)(2,1)}, ...) custom-call(s32[4,512]{1,0:T(4,128)} %ids_own.1, ...), custom_call_target="tpu_custom_call" | custom-call | tf_op jit(solution)/shard_map/stage_pipeline/pallas_call | solution.py:233
  59.2 32.9 %finish.1 = (f32[64,30522]{1,0:T(8,128)}, f32[8,64,512]{2,1,0:T(8,128)}, f32[8,256,128]{2,1,0:T(8,128)}) custom-call(s32[4,512]{1,0:T(4,128)} %ids_own.1, s32[4,512]{1,0:T(4,128)} %get-tuple-element.13.ids_peer, f32[30522,1,128]{2,1,0:T(1,128)} %bitcast.7, f32[30522,1,128]{2,1,0:T(1,128)} %get-tuple-element.14.acc_peer, ...), custom_call_target="tpu_custom_call" | custom-call | tf_op jit(solution)/shard_map/finish/pallas_call | solution.py:271
where the time goes:
time: 92.3 us; the launch traced here: 92.1 us
  Pallas kernels  91.5 us (99%)
    pallas_call x1, Pallas kernels, device_body(): pl.pallas_call(functools.partial(stage_kernel, stages), name='stage_pipel...  58.6 us
    pallas_call x1, Pallas kernels, device_body(): pl.pallas_call(functools.partial(finish_kernel, vocab), name='finish', gr...  32.9 us

commit v1 on v0

--- a/solution.py
+++ b/solution.py
@@ -14,6 +14,7 @@
 C0 = 0.7978845608028654
 C1 = 0.7978845608028654 * 0.044715
 FF_CHUNK = 256
+GROUP = 8
 VOCAB_BLOCK = 2048
 VOCAB_TILE = 256
 
@@ -56,9 +57,21 @@
     cot[...] = d_x.astype(BF16)
 
 
+def mark_repeats(ids):
+    lane = lax.rem(lax.broadcasted_iota(jnp.int32, ids.shape, 1), GROUP)
+    found = jnp.zeros_like(ids)
+    for shift in range(1, GROUP):
+        found = jnp.where((pltpu.roll(ids, shift, 1) == ids) & (lane >= shift), 1, found)
+    shift = 1
+    while shift < GROUP:
+        found = found | pltpu.roll(found, ids.shape[1] - shift, 1)
+        shift *= 2
+    return found
+
+
 def stage_kernel(stages, ids, d_out, stored_x, w_in, w_out, acc_in, acc_out, acc_emb,
-                 ids_peer, acc_peer, dx_all, gi_own, gi_recv, go_own, go_recv,
-                 acts_x, acts_a, acts_s, cot, dx_send, cot_in, sum_in, sum_out_t, acc_o, gi_bf, go_bf,
+                 marks, ids_peer, tab_own, tab_peer, dx_all, gi_own, gi_recv, go_own, go_recv,
+                 acts_x, acts_a, acts_s, cot, dx_send, cot_in, sum_in, sum_out_t, acc_o, mark_own, mark_peer, ids_buf,
                  load_sem, ex_send, ex_recv, cot_send, cot_recv, bc_send, bc_recv, pr_send, pr_recv, loc_sem, g_sem, g_send, g_recv):
     stage = lax.axis_index('pp')
     rep = lax.axis_index('dp')
@@ -75,17 +88,21 @@
     load_out = pltpu.make_async_copy(acc_out, acc_o, load_sem.at[1])
     load_in.start()
     load_out.start()
+    vocab = acc_emb.shape[0]
+    load_emb = pltpu.make_async_copy(acc_emb, tab_own.at[pl.ds(0, vocab)], load_sem.at[2])
+    load_emb.start()
     sum_out_t[...] = jnp.zeros_like(sum_out_t)
 
     def forward(step_id):
         acts_x[0] = stored_x[last - stage - step_id]
         pl.loop(0, layers)(lambda layer_id: forward_layer(layer_id, w_in, w_out, acts_x, acts_a, acts_s))
 
+    mark_own[...] = mark_repeats(ids[...])
     forward(0)
     pl.semaphore_wait(barrier, 2 * stages - 1)
 
-    ex_ids = pltpu.make_async_remote_copy(ids, ids_peer, ex_send.at[0], ex_recv.at[0], device_id=(stage, other), device_id_type=MESH)
-    ex_emb = pltpu.make_async_remote_copy(acc_emb, acc_peer, ex_send.at[1], ex_recv.at[1], device_id=(stage, other), device_id_type=MESH)
+    ex_ids = pltpu.make_async_remote_copy(ids, ids_buf, ex_send.at[0], ex_recv.at[0], device_id=(stage, other), device_id_type=MESH)
+    ex_emb = pltpu.make_async_remote_copy(acc_emb, tab_peer.at[pl.ds(0, vocab)], ex_send.at[1], ex_recv.at[1], device_id=(stage, other), device_id_type=MESH)
     ex_ids.start()
     ex_emb.start()
     load_in.wait()
@@ -133,6 +150,18 @@
                     bc_copy(step_id, target).start()
                 peer_copy(step_id, dx_send.at[step_id]).start()
                 local_copy(step_id).start()
+
+    ex_ids.wait()
+    mark_peer[...] = mark_own[...] | mark_repeats(ids_buf[...])
+    small = [
+        pltpu.make_async_copy(mark_peer, marks, load_sem.at[3]),
+        pltpu.make_async_copy(ids_buf, ids_peer, load_sem.at[4]),
+    ]
+    for copy in small:
+        copy.start()
+
+    gi_bf = acts_a.at[:, pl.ds(0, w_in.shape[1]), :]
+    go_bf = acts_x.at[pl.ds(0, layers)]
 
     @pl.loop(0, layers)
     def _(layer_id):
@@ -173,42 +202,64 @@
         peer_copy(step_id, dx_send.at[step_id]).wait()
     for copy in keep + give:
         copy.wait()
-    ex_ids.wait()
+    for copy in small:
+        copy.wait()
     ex_emb.wait()
-
-
-def finish_kernel(vocab, ids_own, ids_peer, acc_own, acc_peer, dx_all, gi_own, gi_recv, go_own, go_recv,
-                  emb_t, grad_in, grad_out, tab_own, tab_peer, dxf, sems):
+    load_emb.wait()
+
+
+def finish_kernel(ids_own, ids_peer, marks, tab_own, tab_peer, dx_all, gi_own, gi_recv, go_own, go_recv,
+                  emb_t, grad_in, grad_out, dxb, dxf, gi_buf, go_buf, gi_out, go_out, sems):
     step = pl.program_id(0)
     rep = lax.axis_index('dp')
     padded = tab_own.shape[0]
-    rows_own = tab_own.reshape(padded, tab_own.shape[2])
-    rows_peer = tab_peer.reshape(padded, tab_peer.shape[2])
+    width = tab_own.shape[2]
+    rows_own = tab_own.reshape(padded, width)
+    rows_peer = tab_peer.reshape(padded, width)
     micros, tokens = ids_own.shape
+    load_dx = pltpu.make_async_copy(dx_all, dxb, sems.at[0])
+    loads = [pltpu.make_async_copy(src, dst, sems.at[1 + pos]) for pos, (src, dst) in enumerate(
+        ((gi_own, gi_buf.at[0]), (gi_recv, gi_buf.at[1]), (go_own, go_buf.at[0]), (go_recv, go_buf.at[1])))]
+    stores = [pltpu.make_async_copy(gi_out, grad_in, sems.at[5]), pltpu.make_async_copy(go_out, grad_out, sems.at[6])]
 
     @pl.when(step == 0)
     def _():
-        load_own = pltpu.make_async_copy(acc_own, tab_own.at[pl.ds(0, vocab)], sems.at[0])
-        load_peer = pltpu.make_async_copy(acc_peer, tab_peer.at[pl.ds(0, vocab)], sems.at[1])
-        load_own.start()
-        load_peer.start()
-        grad_in[...] = (gi_own[...].astype(F32) + gi_recv[...].astype(F32)) * 0.5
-        grad_out[...] = (go_own[...].astype(F32) + go_recv[...].astype(F32)) * 0.5
-        dxf[0] = dx_all[rep].astype(F32)
-        dxf[1] = dx_all[1 - rep].astype(F32)
-        load_own.wait()
-        load_peer.wait()
+        load_dx.start()
+        for copy in loads:
+            copy.start()
+        load_dx.wait()
+        dxf[0] = dxb[rep].astype(F32)
+        dxf[1] = dxb[1 - rep].astype(F32)
+        tables = ((ids_own, rows_own, 0), (ids_peer, rows_peer, 1))
         for micro in range(micros):
-            def add_rows(row, carry):
-                first = ids_own[micro, row]
-                second = ids_peer[micro, row]
-                rows_own[pl.ds(first, 1), :] = rows_own[pl.ds(first, 1), :] + dxf[0, micro, pl.ds(row, 1), :]
-                rows_peer[pl.ds(second, 1), :] = rows_peer[pl.ds(second, 1), :] + dxf[1, micro, pl.ds(row, 1), :]
+            def add_group(group, carry):
+                base = pl.multiple_of(group * GROUP, GROUP)
+                repeated = marks[micro, base] != 0
+
+                @pl.when(repeated)
+                def _():
+                    for ids, rows, side in tables:
+                        for pos in range(GROUP):
+                            row = ids[micro, base + pos]
+                            rows[pl.ds(row, 1), :] = rows[pl.ds(row, 1), :] + dxf[side, micro, pl.ds(base + pos, 1), :]
+
+                @pl.when(jnp.logical_not(repeated))
+                def _():
+                    for ids, rows, side in tables:
+                        places = [ids[micro, base + pos] for pos in range(GROUP)]
+                        sums = [rows[pl.ds(places[pos], 1), :] + dxf[side, micro, pl.ds(base + pos, 1), :] for pos in range(GROUP)]
+                        for pos in range(GROUP):
+                            rows[pl.ds(places[pos], 1), :] = sums[pos]
                 return carry
-            lax.fori_loop(0, tokens, add_rows, 0, unroll=8)
+            lax.fori_loop(0, tokens // GROUP, add_group, 0)
+        for copy in loads:
+            copy.wait()
+        gi_out[...] = (gi_buf[0].astype(F32) + gi_buf[1].astype(F32)) * 0.5
+        go_out[...] = (go_buf[0].astype(F32) + go_buf[1].astype(F32)) * 0.5
+        for copy in stores:
+            copy.start()
 
     half = emb_t.shape[0]
-    width = tab_own.shape[2]
     row_id = lax.broadcasted_iota(jnp.int32, (half, 2 * width), 0)
     col_id = lax.broadcasted_iota(jnp.int32, (half, 2 * width), 1)
     pick = jnp.where(lax.rem(col_id, width) == row_id + half * rep, 0.5, 0.0).astype(BF16)
@@ -217,6 +268,11 @@
         both = jnp.concatenate([rows_own[pl.ds(first, VOCAB_TILE), :].astype(BF16), rows_peer[pl.ds(first, VOCAB_TILE), :].astype(BF16)], axis=1)
         emb_t[:, start:start + VOCAB_TILE] = lax.dot_general(pick, both, NT, preferred_element_type=F32)
 
+    @pl.when(step == pl.num_programs(0) - 1)
+    def _():
+        for copy in stores:
+            copy.wait()
+
 
 def solution(mesh):
     stages = mesh.shape['pp']
@@ -227,17 +283,20 @@
         vocab = acc_emb.shape[1]
         half_i, half_o, half_e = hid // 2, ff // 2, hid // 2
         emb_rows = acc_emb.reshape(vocab, 1, hid)
-        any_spec = pl.BlockSpec(memory_space=pl.ANY)
+        table = pltpu.VMEM((pl.cdiv(vocab, VOCAB_BLOCK) * VOCAB_BLOCK, 1, hid), F32)
+        any_spec = pl.BlockSpec(memory_space=pltpu.HBM)
         vmem_spec = pl.BlockSpec(memory_space=pltpu.VMEM)
         dma = pltpu.SemaphoreType.DMA
-        ids_peer, acc_peer, dx_all, gi_own, gi_recv, go_own, go_recv = pl.pallas_call(
+        marks, ids_peer, tab_own, tab_peer, dx_all, gi_own, gi_recv, go_own, go_recv = pl.pallas_call(
             functools.partial(stage_kernel, stages),
             name='stage_pipeline',
-            in_specs=[any_spec] + [vmem_spec] * 4 + [any_spec] * 3,
-            out_specs=[any_spec] * 7,
+            in_specs=[vmem_spec] * 5 + [any_spec] * 3,
+            out_specs=[any_spec] * 2 + [vmem_spec] * 2 + [any_spec] * 5,
             out_shape=[
                 jax.ShapeDtypeStruct(tok_ids.shape, tok_ids.dtype),
-                jax.ShapeDtypeStruct((vocab, 1, hid), F32),
+                jax.ShapeDtypeStruct(tok_ids.shape, tok_ids.dtype),
+                table,
+                table,
                 jax.ShapeDtypeStruct((2, stages, tokens, hid), BF16),
                 jax.ShapeDtypeStruct((layers, half_i, ff), BF16),
                 jax.ShapeDtypeStruct((layers, half_i, ff), BF16),
@@ -254,39 +313,42 @@
                 pltpu.VMEM((layers, hid, ff), F32),
                 pltpu.VMEM((layers, hid, ff), F32),
                 pltpu.VMEM((layers, ff, hid), F32),
-                pltpu.VMEM((layers, hid, ff), BF16),
-                pltpu.VMEM((layers, ff, hid), BF16),
-                dma((2,)), dma((2,)), dma((2,)),
+                pltpu.VMEM(tok_ids.shape, jnp.int32),
+                pltpu.VMEM(tok_ids.shape, jnp.int32),
+                pltpu.VMEM(tok_ids.shape, jnp.int32),
+                dma((5,)), dma((2,)), dma((2,)),
                 dma((stages,)), dma((stages,)),
                 dma((stages, stages)), dma((stages,)),
                 dma((stages,)), dma((stages,)), dma((stages,)),
                 dma((2,)), dma((2,)), dma((2,)),
             ],
-            compiler_params=pltpu.CompilerParams(collective_id=0, has_side_effects=True, vmem_limit_bytes=60 * 2**20),
+            compiler_params=pltpu.CompilerParams(collective_id=0, has_side_effects=True, vmem_limit_bytes=28 * 2**20),
         )(tok_ids, d_out[0], stored_x[0], w_in, w_out, acc_in[:, 0], acc_out[:, 0], emb_rows)
 
-        padded = pl.cdiv(vocab, VOCAB_BLOCK) * VOCAB_BLOCK
-        whole = lambda shape: pl.BlockSpec(shape, lambda step: (0,) * len(shape))
+        resident = lambda x: pltpu.with_memory_space_constraint(x, pltpu.VMEM)
         smem_spec = pl.BlockSpec(memory_space=pltpu.SMEM)
         emb_t, grad_in, grad_out = pl.pallas_call(
-            functools.partial(finish_kernel, vocab),
+            finish_kernel,
             name='finish',
             grid=(pl.cdiv(vocab, VOCAB_BLOCK),),
-            in_specs=[smem_spec] * 2 + [any_spec] * 2 + [whole(v.shape) for v in (dx_all, gi_own, gi_recv, go_own, go_recv)],
-            out_specs=[pl.BlockSpec((half_e, VOCAB_BLOCK), lambda step: (0, step)), whole((layers, half_i, ff)), whole((layers, half_o, hid))],
+            in_specs=[smem_spec] * 3 + [vmem_spec] * 2 + [any_spec] * 5,
+            out_specs=[pl.BlockSpec((half_e, VOCAB_BLOCK), lambda step: (0, step))] + [any_spec] * 2,
             out_shape=[
                 jax.ShapeDtypeStruct((half_e, vocab), F32),
                 jax.ShapeDtypeStruct((layers, half_i, ff), F32),
                 jax.ShapeDtypeStruct((layers, half_o, hid), F32),
             ],
             scratch_shapes=[
-                pltpu.VMEM((padded, 1, hid), F32),
-                pltpu.VMEM((padded, 1, hid), F32),
+                pltpu.VMEM((2, stages, tokens, hid), BF16),
                 pltpu.VMEM((2, stages, tokens, hid), F32),
-                dma((2,)),
+                pltpu.VMEM((2, layers, half_i, ff), BF16),
+                pltpu.VMEM((2, layers, half_o, hid), BF16),
+                pltpu.VMEM((layers, half_i, ff), F32),
+                pltpu.VMEM((layers, half_o, hid), F32),
+                dma((7,)),
             ],
-            compiler_params=pltpu.CompilerParams(vmem_limit_bytes=60 * 2**20),
-        )(tok_ids, ids_peer, emb_rows, acc_peer, dx_all, gi_own, gi_recv, go_own, go_recv)
+            compiler_params=pltpu.CompilerParams(vmem_limit_bytes=28 * 2**20),
+        )(tok_ids, ids_peer, marks, resident(tab_own), resident(tab_peer), dx_all, gi_own, gi_recv, go_own, go_recv)
         return grad_in, grad_out, emb_t.T
 
     return jax.shard_map(device_body, mesh=mesh, in_specs=(P(None, 'dp'), P('pp', 'dp', None), P('pp', None, 'dp', None), P('pp', None, None), P('pp', None, None), P('pp', 'dp', None, None), P('pp', 'dp', None, None), P('dp', None, None)), out_specs=(P('pp', 'dp', None), P('pp', 'dp', None), P(None, 'dp')), check_vma=False)

time: 92.3 us -> 84.7 us (0.918)
  Pallas kernels: 91.5 us -> 83.8 us
    pallas_call x1, Pallas kernels: 32.9 us -> 25 us  [device_body(): pl.pallas_call(finish_kernel, name='finish', grid=(pl.cdiv(vocab, VOCAB_B...]
where the time goes in v1:
time: 84.7 us; the launch traced here: 84.5 us
  Pallas kernels  83.8 us (99%)
    pallas_call x1, Pallas kernels, device_body(): pl.pallas_call(functools.partial(stage_kernel, stages), name='stage_pipel...  58.9 us
    pallas_call x1, Pallas kernels, device_body(): pl.pallas_call(finish_kernel, name='finish', grid=(pl.cdiv(vocab, VOCAB_B...  25 us

profile of v1, /device:TPU:7, one launch (start us, length us, event | category | flops | bytes accessed | tf_op | source)
XLA Modules:
  0.0 84.5 jit_solution(1197483469617726417)
XLA Ops:
  0.6 58.9 %stage_pipeline.1 = (s32[4,512]{1,0:T(4,128)}, s32[4,512]{1,0:T(4,128)}, f32[30720,1,128]{2,1,0:T(1,128)S(1)}, f32[30720,1,128]{2,1,0:T(1,128)S(1)}, bf16[2,4,51...) custom-call(s32[4,512]{1,0:T(4,128)} %ids_own.1, ...), custom_call_target="tpu_custom_call" | custom-call | tf_op jit(solution)/shard_map/stage_pipeline/pallas_call | solution.py:290
  59.5 25.0 %finish.1 = (f32[64,30522]{1,0:T(8,128)}, f32[8,64,512]{2,1,0:T(8,128)}, f32[8,256,128]{2,1,0:T(8,128)}) custom-call(s32[4,512]{1,0:T(4,128)} %ids_own.1, s32[4,512]{1,0:T(4,128)} %get-tuple-element.15.ids_peer, s32[4,512]{1,0:T(4,128)} %get-tuple-element.16.marks, f32[30720,1,128]{2,1,0:T(1,128)S(1)} %get-tuple-element.17.tab_own, ...), custom_call_target="tpu_custom_call" | custom-call | tf_op jit(solution)/shard_map/finish/pallas_call | solution.py:330

commit v2 on v1

--- a/solution.py
+++ b/solution.py
@@ -14,8 +14,10 @@
 C0 = 0.7978845608028654
 C1 = 0.7978845608028654 * 0.044715
 FF_CHUNK = 256
-GROUP = 8
-VOCAB_BLOCK = 2048
+GROUP = 32
+BATCH = 2
+LANES = 128
+VOCAB_BLOCK = 5120
 VOCAB_TILE = 256
 
 
@@ -70,8 +72,8 @@
 
 
 def stage_kernel(stages, ids, d_out, stored_x, w_in, w_out, acc_in, acc_out, acc_emb,
-                 marks, ids_peer, tab_own, tab_peer, dx_all, gi_own, gi_recv, go_own, go_recv,
-                 acts_x, acts_a, acts_s, cot, dx_send, cot_in, sum_in, sum_out_t, acc_o, mark_own, mark_peer, ids_buf,
+                 marks, ids_own, ids_peer, tab_own, tab_peer, dx_all, gi_own, gi_recv, go_own, go_recv,
+                 acts_x, acts_a, acts_s, cot, dx_send, cot_in, sum_in, sum_out_t, acc_o, mark_buf, ids_mine, ids_buf,
                  load_sem, ex_send, ex_recv, cot_send, cot_recv, bc_send, bc_recv, pr_send, pr_recv, loc_sem, g_sem, g_send, g_recv):
     stage = lax.axis_index('pp')
     rep = lax.axis_index('dp')
@@ -97,11 +99,13 @@
         acts_x[0] = stored_x[last - stage - step_id]
         pl.loop(0, layers)(lambda layer_id: forward_layer(layer_id, w_in, w_out, acts_x, acts_a, acts_s))
 
-    mark_own[...] = mark_repeats(ids[...])
+    micros, tokens = ids.shape
+    for block in range(tokens // LANES):
+        ids_mine[pl.ds(block * micros, micros), :] = ids[:, pl.ds(block * LANES, LANES)]
     forward(0)
     pl.semaphore_wait(barrier, 2 * stages - 1)
 
-    ex_ids = pltpu.make_async_remote_copy(ids, ids_buf, ex_send.at[0], ex_recv.at[0], device_id=(stage, other), device_id_type=MESH)
+    ex_ids = pltpu.make_async_remote_copy(ids_mine, ids_buf, ex_send.at[0], ex_recv.at[0], device_id=(stage, other), device_id_type=MESH)
     ex_emb = pltpu.make_async_remote_copy(acc_emb, tab_peer.at[pl.ds(0, vocab)], ex_send.at[1], ex_recv.at[1], device_id=(stage, other), device_id_type=MESH)
     ex_ids.start()
     ex_emb.start()
@@ -152,10 +156,11 @@
                 local_copy(step_id).start()
 
     ex_ids.wait()
-    mark_peer[...] = mark_own[...] | mark_repeats(ids_buf[...])
+    mark_buf[...] = mark_repeats(ids_mine[...]) | mark_repeats(ids_buf[...])
     small = [
-        pltpu.make_async_copy(mark_peer, marks, load_sem.at[3]),
+        pltpu.make_async_copy(mark_buf, marks, load_sem.at[3]),
         pltpu.make_async_copy(ids_buf, ids_peer, load_sem.at[4]),
+        pltpu.make_async_copy(ids_mine, ids_own, load_sem.at[5]),
     ]
     for copy in small:
         copy.start()
@@ -209,49 +214,65 @@
 
 
 def finish_kernel(ids_own, ids_peer, marks, tab_own, tab_peer, dx_all, gi_own, gi_recv, go_own, go_recv,
-                  emb_t, grad_in, grad_out, dxb, dxf, gi_buf, go_buf, gi_out, go_out, sems):
+                  emb_t, grad_in, grad_out, dxf, gi_buf, go_buf, gi_out, go_out, sems):
     step = pl.program_id(0)
     rep = lax.axis_index('dp')
     padded = tab_own.shape[0]
     width = tab_own.shape[2]
     rows_own = tab_own.reshape(padded, width)
     rows_peer = tab_peer.reshape(padded, width)
-    micros, tokens = ids_own.shape
-    load_dx = pltpu.make_async_copy(dx_all, dxb, sems.at[0])
-    loads = [pltpu.make_async_copy(src, dst, sems.at[1 + pos]) for pos, (src, dst) in enumerate(
+    micros = dx_all.shape[1]
+    loads = [pltpu.make_async_copy(src, dst, sems.at[pos]) for pos, (src, dst) in enumerate(
         ((gi_own, gi_buf.at[0]), (gi_recv, gi_buf.at[1]), (go_own, go_buf.at[0]), (go_recv, go_buf.at[1])))]
-    stores = [pltpu.make_async_copy(gi_out, grad_in, sems.at[5]), pltpu.make_async_copy(go_out, grad_out, sems.at[6])]
+    stores = [pltpu.make_async_copy(gi_out, grad_in, sems.at[4]), pltpu.make_async_copy(go_out, grad_out, sems.at[5])]
 
     @pl.when(step == 0)
     def _():
-        load_dx.start()
         for copy in loads:
             copy.start()
-        load_dx.wait()
-        dxf[0] = dxb[rep].astype(F32)
-        dxf[1] = dxb[1 - rep].astype(F32)
-        tables = ((ids_own, rows_own, 0), (ids_peer, rows_peer, 1))
-        for micro in range(micros):
-            def add_group(group, carry):
+        dxf[0] = dx_all[rep].astype(F32)
+        dxf[1] = dx_all[1 - rep].astype(F32)
+        sides = ((ids_own, rows_own, 0), (ids_peer, rows_peer, 1))
+
+        @pl.loop(0, ids_own.shape[0])
+        def _(line):
+            micro = lax.rem(line, micros)
+            token = (line // micros) * LANES
+
+            @pl.loop(0, LANES // GROUP)
+            def _(group):
                 base = pl.multiple_of(group * GROUP, GROUP)
-                repeated = marks[micro, base] != 0
+                repeated = marks[line, base] != 0
 
                 @pl.when(repeated)
                 def _():
-                    for ids, rows, side in tables:
-                        for pos in range(GROUP):
-                            row = ids[micro, base + pos]
-                            rows[pl.ds(row, 1), :] = rows[pl.ds(row, 1), :] + dxf[side, micro, pl.ds(base + pos, 1), :]
+                    @pl.loop(0, GROUP)
+                    def _(pos):
+                        for ids, rows, side in sides:
+                            row = pl.ds(ids[line, base + pos], 1)
+                            rows[row, :] = rows[row, :] + dxf[side, micro, pl.ds(token + base + pos, 1), :]
 
                 @pl.when(jnp.logical_not(repeated))
                 def _():
-                    for ids, rows, side in tables:
-                        places = [ids[micro, base + pos] for pos in range(GROUP)]
-                        sums = [rows[pl.ds(places[pos], 1), :] + dxf[side, micro, pl.ds(base + pos, 1), :] for pos in range(GROUP)]
-                        for pos in range(GROUP):
-                            rows[pl.ds(places[pos], 1), :] = sums[pos]
-                return carry
-            lax.fori_loop(0, tokens // GROUP, add_group, 0)
+                    def add_batch(start):
+                        sums = []
+                        for ids, rows, side in sides:
+                            for pos in range(start, start + BATCH):
+                                row = pl.ds(ids[line, base + pos], 1)
+                                sums.append((rows, row, rows[row, :] + dxf[side, micro, pl.ds(token + base + pos, 1), :]))
+                        return sums
+
+                    def store_batch(sums):
+                        for rows, row, value in sums:
+                            rows[row, :] = value
+
+                    held = add_batch(0)
+                    for start in range(BATCH, GROUP, BATCH):
+                        fresh = add_batch(start)
+                        store_batch(held)
+                        held = fresh
+                    store_batch(held)
+
         for copy in loads:
             copy.wait()
         gi_out[...] = (gi_buf[0].astype(F32) + gi_buf[1].astype(F32)) * 0.5
@@ -283,21 +304,23 @@
         vocab = acc_emb.shape[1]
         half_i, half_o, half_e = hid // 2, ff // 2, hid // 2
         emb_rows = acc_emb.reshape(vocab, 1, hid)
+        lines = jax.ShapeDtypeStruct((tok_ids.size // LANES, LANES), tok_ids.dtype)
         table = pltpu.VMEM((pl.cdiv(vocab, VOCAB_BLOCK) * VOCAB_BLOCK, 1, hid), F32)
         any_spec = pl.BlockSpec(memory_space=pltpu.HBM)
         vmem_spec = pl.BlockSpec(memory_space=pltpu.VMEM)
         dma = pltpu.SemaphoreType.DMA
-        marks, ids_peer, tab_own, tab_peer, dx_all, gi_own, gi_recv, go_own, go_recv = pl.pallas_call(
+        marks, ids_own, ids_peer, tab_own, tab_peer, dx_all, gi_own, gi_recv, go_own, go_recv = pl.pallas_call(
             functools.partial(stage_kernel, stages),
             name='stage_pipeline',
             in_specs=[vmem_spec] * 5 + [any_spec] * 3,
-            out_specs=[any_spec] * 2 + [vmem_spec] * 2 + [any_spec] * 5,
+            out_specs=[any_spec] * 3 + [vmem_spec] * 3 + [any_spec] * 4,
             out_shape=[
-                jax.ShapeDtypeStruct(tok_ids.shape, tok_ids.dtype),
-                jax.ShapeDtypeStruct(tok_ids.shape, tok_ids.dtype),
+                lines,
+                lines,
+                lines,
                 table,
                 table,
-                jax.ShapeDtypeStruct((2, stages, tokens, hid), BF16),
+                pltpu.VMEM((2, stages, tokens, hid), BF16),
                 jax.ShapeDtypeStruct((layers, half_i, ff), BF16),
                 jax.ShapeDtypeStruct((layers, half_i, ff), BF16),
                 jax.ShapeDtypeStruct((layers, half_o, hid), BF16),
@@ -313,10 +336,10 @@
                 pltpu.VMEM((layers, hid, ff), F32),
                 pltpu.VMEM((layers, hid, ff), F32),
                 pltpu.VMEM((layers, ff, hid), F32),
-                pltpu.VMEM(tok_ids.shape, jnp.int32),
-                pltpu.VMEM(tok_ids.shape, jnp.int32),
-                pltpu.VMEM(tok_ids.shape, jnp.int32),
-                dma((5,)), dma((2,)), dma((2,)),
+                pltpu.VMEM(lines.shape, jnp.int32),
+                pltpu.VMEM(lines.shape, jnp.int32),
+                pltpu.VMEM(lines.shape, jnp.int32),
+                dma((6,)), dma((2,)), dma((2,)),
                 dma((stages,)), dma((stages,)),
                 dma((stages, stages)), dma((stages,)),
                 dma((stages,)), dma((stages,)), dma((stages,)),
@@ -331,7 +354,7 @@
             finish_kernel,
             name='finish',
             grid=(pl.cdiv(vocab, VOCAB_BLOCK),),
-            in_specs=[smem_spec] * 3 + [vmem_spec] * 2 + [any_spec] * 5,
+            in_specs=[smem_spec] * 3 + [vmem_spec] * 3 + [any_spec] * 4,
             out_specs=[pl.BlockSpec((half_e, VOCAB_BLOCK), lambda step: (0, step))] + [any_spec] * 2,
             out_shape=[
                 jax.ShapeDtypeStruct((half_e, vocab), F32),
@@ -339,16 +362,15 @@
                 jax.ShapeDtypeStruct((layers, half_o, hid), F32),
             ],
             scratch_shapes=[
-                pltpu.VMEM((2, stages, tokens, hid), BF16),
                 pltpu.VMEM((2, stages, tokens, hid), F32),
                 pltpu.VMEM((2, layers, half_i, ff), BF16),
                 pltpu.VMEM((2, layers, half_o, hid), BF16),
                 pltpu.VMEM((layers, half_i, ff), F32),
                 pltpu.VMEM((layers, half_o, hid), F32),
-                dma((7,)),
+                dma((6,)),
             ],
             compiler_params=pltpu.CompilerParams(vmem_limit_bytes=28 * 2**20),
-        )(tok_ids, ids_peer, marks, resident(tab_own), resident(tab_peer), dx_all, gi_own, gi_recv, go_own, go_recv)
+        )(ids_own, ids_peer, marks, resident(tab_own), resident(tab_peer), resident(dx_all), gi_own, gi_recv, go_own, go_recv)
         return grad_in, grad_out, emb_t.T
 
     return jax.shard_map(device_body, mesh=mesh, in_specs=(P(None, 'dp'), P('pp', 'dp', None), P('pp', None, 'dp', None), P('pp', None, None), P('pp', None, None), P('pp', 'dp', None, None), P('pp', 'dp', None, None), P('dp', None, None)), out_specs=(P('pp', 'dp', None), P('pp', 'dp', None), P(None, 'dp')), check_vma=False)

time: 84.7 us -> 76 us (0.90)
  Pallas kernels: 83.8 us -> 75.2 us
    pallas_call x1, Pallas kernels: 25 us -> 16.3 us  [device_body(): pl.pallas_call(finish_kernel, name='finish', grid=(pl.cdiv(vocab, VOCAB_B...]
where the time goes in v2:
time: 76 us; the launch traced here: 75.8 us
  Pallas kernels  75.2 us (99%)
    pallas_call x1, Pallas kernels, device_body(): pl.pallas_call(functools.partial(stage_kernel, stages), name='stage_pipel...  58.9 us
    pallas_call x1, Pallas kernels, device_body(): pl.pallas_call(finish_kernel, name='finish', grid=(pl.cdiv(vocab, VOCAB_B...  16.3 us

profile of v2, /device:TPU:7, one launch (start us, length us, event | category | flops | bytes accessed | tf_op | source)
XLA Modules:
  0.0 75.8 jit_solution(9576753922798305645)
XLA Ops:
  0.6 58.9 %stage_pipeline.1 = (s32[16,128]{1,0:T(8,128)}, s32[16,128]{1,0:T(8,128)}, s32[16,128]{1,0:T(8,128)}, f32[30720,1,128]{2,1,0:T(1,128)S(1)}, f32[30720,1,128]{2,1...) custom-call(s32[4,512]{1,0:T(4,128)} %ids.1, ...), custom_call_target="tpu_custom_call" | custom-call | tf_op jit(solution)/shard_map/stage_pipeline/pallas_call | solution.py:312
  59.5 16.3 %finish.1 = (f32[64,30522]{1,0:T(8,128)}, f32[8,64,512]{2,1,0:T(8,128)}, f32[8,256,128]{2,1,0:T(8,128)}) custom-call(s32[16,128]{1,0:T(8,128)} %get-tuple-element.16.ids_own, s32[16,128]{1,0:T(8,128)} %get-tuple-element.17.ids_peer, s32[16,128]{1,0:T(8,128)} %get-tuple-element.18.marks, f32[30720,1,128]{2,1,0:T(1,128)S(1)} %get-tuple-element.19.tab_own, ...), custom_call_target="tpu_custom_call" | custom-call | tf_op jit(solution)/shard_map/finish/pallas_call | solution.py:353

commit v3 on v2

--- a/solution.py
+++ b/solution.py
@@ -14,6 +14,8 @@
 C0 = 0.7978845608028654
 C1 = 0.7978845608028654 * 0.044715
 FF_CHUNK = 256
+STRIDE = 8
+PARTS = 2
 GROUP = 32
 BATCH = 2
 LANES = 128
@@ -30,33 +32,47 @@
     return value, slope
 
 
-def forward_layer(layer_id, w_in, w_out, acts_x, acts_a, acts_s):
-    x_cur = acts_x[layer_id]
+def forward_layer(layer_id, rows, w_in, w_out, acts_x, acts_a, acts_s):
+    x_cur = acts_x[layer_id, rows, :]
     out_x = x_cur.astype(F32)
     for start in range(0, w_in.shape[2], FF_CHUNK):
         cols = pl.ds(start, FF_CHUNK)
         pre_act = jnp.dot(x_cur, w_in[layer_id, :, cols], preferred_element_type=F32).astype(BF16)
         value, slope = gelu_parts(pre_act.astype(F32))
         hidden = value.astype(BF16)
-        acts_a[layer_id, :, cols] = hidden
-        acts_s[layer_id, :, cols] = slope
+        acts_a[layer_id, rows, cols] = hidden
+        acts_s[layer_id, rows, cols] = slope
         out_x += jnp.dot(hidden, w_out[layer_id, cols, :], preferred_element_type=F32)
-    acts_x[layer_id + 1] = out_x.astype(BF16)
-
-
-def backward_layer(layer_id, w_in, w_out, acts_x, acts_a, acts_s, cot, sum_in, sum_out_t):
-    cot_cur = cot[...]
-    cot_t = cot_cur.T
-    x_t = acts_x[layer_id].T
+    acts_x[layer_id + 1, rows, :] = out_x.astype(BF16)
+
+
+def backward_layer(layer_id, rows, w_in, w_out, acts_x, acts_a, acts_s, cot, sum_in, sum_out_t):
+    cot_cur = cot[rows, :]
     d_x = cot_cur.astype(F32)
+    d_pres = []
     for start in range(0, w_in.shape[2], FF_CHUNK):
         cols = pl.ds(start, FF_CHUNK)
         d_hidden = lax.dot_general(cot_cur, w_out[layer_id, cols, :], NT, preferred_element_type=F32).astype(BF16)
-        d_pre = (d_hidden.astype(F32) * acts_s[layer_id, :, cols]).astype(BF16)
+        d_pre = (d_hidden.astype(F32) * acts_s[layer_id, rows, cols]).astype(BF16)
+        d_pres.append(d_pre)
         d_x += lax.dot_general(d_pre, w_in[layer_id, :, cols], NT, preferred_element_type=F32)
-        sum_out_t[layer_id, :, cols] += jnp.dot(cot_t, acts_a[layer_id, :, cols], preferred_element_type=F32)
+    cot[rows, :] = d_x.astype(BF16)
+    cot_t = cot_cur.T
+    x_t = acts_x[layer_id, rows, :].T
+    for start, d_pre in zip(range(0, w_in.shape[2], FF_CHUNK), d_pres):
+        cols = pl.ds(start, FF_CHUNK)
+        sum_out_t[layer_id, :, cols] += jnp.dot(cot_t, acts_a[layer_id, rows, cols], preferred_element_type=F32)
         sum_in[layer_id, :, cols] += jnp.dot(x_t, d_pre, preferred_element_type=F32)
-    cot[...] = d_x.astype(BF16)
+
+
+def each_layer(layers, tokens, step):
+    part = tokens // PARTS
+
+    @pl.loop(0, layers // STRIDE)
+    def _(turn):
+        for pos in range(STRIDE):
+            for index in range(PARTS):
+                step(turn * STRIDE + pos, pl.ds(index * part, part))
 
 
 def mark_repeats(ids):
@@ -97,20 +113,13 @@
 
     def forward(step_id):
         acts_x[0] = stored_x[last - stage - step_id]
-        pl.loop(0, layers)(lambda layer_id: forward_layer(layer_id, w_in, w_out, acts_x, acts_a, acts_s))
+        each_layer(layers, tokens, lambda layer_id, rows: forward_layer(layer_id, rows, w_in, w_out, acts_x, acts_a, acts_s))
 
     micros, tokens = ids.shape
     for block in range(tokens // LANES):
         ids_mine[pl.ds(block * micros, micros), :] = ids[:, pl.ds(block * LANES, LANES)]
-    forward(0)
-    pl.semaphore_wait(barrier, 2 * stages - 1)
-
     ex_ids = pltpu.make_async_remote_copy(ids_mine, ids_buf, ex_send.at[0], ex_recv.at[0], device_id=(stage, other), device_id_type=MESH)
     ex_emb = pltpu.make_async_remote_copy(acc_emb, tab_peer.at[pl.ds(0, vocab)], ex_send.at[1], ex_recv.at[1], device_id=(stage, other), device_id_type=MESH)
-    ex_ids.start()
-    ex_emb.start()
-    load_in.wait()
-    load_out.wait()
 
     def cot_copy(step_id):
         return pltpu.make_async_remote_copy(dx_send.at[step_id], cot_in.at[step_id], cot_send.at[step_id], cot_recv.at[step_id],
@@ -131,17 +140,23 @@
     def _(step_id):
         @pl.when(stage + step_id <= last)
         def _():
+            forward(step_id)
+
             @pl.when(step_id == 0)
             def _():
+                pl.semaphore_wait(barrier, 2 * stages - 1)
+                ex_ids.start()
+                ex_emb.start()
+                load_in.wait()
+                load_out.wait()
                 cot[...] = d_out[...]
 
             @pl.when(step_id > 0)
             def _():
-                forward(step_id)
                 cot_copy(step_id - 1).wait_recv()
                 cot[...] = cot_in[step_id - 1]
 
-            pl.loop(0, layers)(lambda back_id: backward_layer(layers - 1 - back_id, w_in, w_out, acts_x, acts_a, acts_s, cot, sum_in, sum_out_t))
+            each_layer(layers, tokens, lambda back_id, rows: backward_layer(layers - 1 - back_id, rows, w_in, w_out, acts_x, acts_a, acts_s, cot, sum_in, sum_out_t))
             dx_send[step_id] = cot[...]
 
             @pl.when(stage > 0)

time: 76 us -> 64.6 us (0.85)
  Pallas kernels: 75.2 us -> 63.8 us
    pallas_call x1, Pallas kernels: 58.9 us -> 47.5 us  [device_body(): pl.pallas_call(functools.partial(stage_kernel, stages), name='stage_pipel...]
where the time goes in v3:
time: 64.6 us; the launch traced here: 64.5 us
  Pallas kernels  63.8 us (99%)
    pallas_call x1, Pallas kernels, device_body(): pl.pallas_call(functools.partial(stage_kernel, stages), name='stage_pipel...  47.5 us
    pallas_call x1, Pallas kernels, device_body(): pl.pallas_call(finish_kernel, name='finish', grid=(pl.cdiv(vocab, VOCAB_B...  16.3 us

profile of v3, /device:TPU:7, one launch (start us, length us, event | category | flops | bytes accessed | tf_op | source)
XLA Modules:
  0.0 64.5 jit_solution(3725234652689841943)
XLA Ops:
  0.6 47.5 %stage_pipeline.1 = (s32[16,128]{1,0:T(8,128)}, s32[16,128]{1,0:T(8,128)}, s32[16,128]{1,0:T(8,128)}, f32[30720,1,128]{2,1,0:T(1,128)S(1)}, f32[30720,1,128]{2,1...) custom-call(s32[4,512]{1,0:T(4,128)} %ids.1, ...), custom_call_target="tpu_custom_call" | custom-call | tf_op jit(solution)/shard_map/stage_pipeline/pallas_call | solution.py:327
  48.2 16.3 %finish.1 = (f32[64,30522]{1,0:T(8,128)}, f32[8,64,512]{2,1,0:T(8,128)}, f32[8,256,128]{2,1,0:T(8,128)}) custom-call(s32[16,128]{1,0:T(8,128)} %get-tuple-element.16.ids_own, s32[16,128]{1,0:T(8,128)} %get-tuple-element.17.ids_peer, s32[16,128]{1,0:T(8,128)} %get-tuple-element.18.marks, f32[30720,1,128]{2,1,0:T(1,128)S(1)} %get-tuple-element.19.tab_own, ...), custom_call_target="tpu_custom_call" | custom-call | tf_op jit(solution)/shard_map/finish/pallas_call | solution.py:368

commit v4 on v3

--- a/solution.py
+++ b/solution.py
@@ -14,65 +14,66 @@
 C0 = 0.7978845608028654
 C1 = 0.7978845608028654 * 0.044715
 FF_CHUNK = 256
-STRIDE = 8
-PARTS = 2
+FORWARD_PARTS = 2
+BACKWARD_PARTS = 1
 GROUP = 32
 BATCH = 2
 LANES = 128
+CHUNKS = 4
+ROUTES = {1: (0, 1, 2, 3), 2: (2, 3, 0, 1), 3: (0, 2, 1, 3)}
 VOCAB_BLOCK = 5120
 VOCAB_TILE = 256
 
 
-def gelu_parts(pre_act):
-    square = pre_act * pre_act
-    tanh_val = jnp.tanh(pre_act * (C0 + C1 * square))
-    half = 0.5 + 0.5 * tanh_val
-    value = pre_act * half
-    slope = half + (value - value * half) * (2.0 * C0 + (6.0 * C1) * square)
+def gelu_parts(half_act):
+    cubic = (8.0 * C1) * (half_act * half_act)
+    tanh_val = jnp.tanh(half_act * (2.0 * C0 + cubic))
+    upper = 1.0 + tanh_val
+    value = half_act * upper
+    slope = upper + (value * (1.0 - tanh_val)) * (2.0 * C0 + 3.0 * cubic)
     return value, slope
 
 
-def forward_layer(layer_id, rows, w_in, w_out, acts_x, acts_a, acts_s):
+def forward_layer(layer_id, rows, final, w_half, w_out, acts_x, acts_a, acts_s):
     x_cur = acts_x[layer_id, rows, :]
     out_x = x_cur.astype(F32)
-    for start in range(0, w_in.shape[2], FF_CHUNK):
+    for start in range(0, w_half.shape[2], FF_CHUNK):
         cols = pl.ds(start, FF_CHUNK)
-        pre_act = jnp.dot(x_cur, w_in[layer_id, :, cols], preferred_element_type=F32).astype(BF16)
-        value, slope = gelu_parts(pre_act.astype(F32))
+        half_act = jnp.dot(x_cur, w_half[layer_id, :, cols], preferred_element_type=F32).astype(BF16)
+        value, slope = gelu_parts(half_act.astype(F32))
         hidden = value.astype(BF16)
         acts_a[layer_id, rows, cols] = hidden
         acts_s[layer_id, rows, cols] = slope
-        out_x += jnp.dot(hidden, w_out[layer_id, cols, :], preferred_element_type=F32)
-    acts_x[layer_id + 1, rows, :] = out_x.astype(BF16)
-
-
-def backward_layer(layer_id, rows, w_in, w_out, acts_x, acts_a, acts_s, cot, sum_in, sum_out_t):
+        if not final:
+            out_x += jnp.dot(hidden, w_out[layer_id, cols, :], preferred_element_type=F32)
+    if not final:
+        acts_x[layer_id + 1, rows, :] = out_x.astype(BF16)
+
+
+def backward_layer(layer_id, rows, w_half, w_out, acts_x, acts_a, acts_s, cot, sum_in, sum_out_t):
     cot_cur = cot[rows, :]
     d_x = cot_cur.astype(F32)
     d_pres = []
-    for start in range(0, w_in.shape[2], FF_CHUNK):
+    for start in range(0, w_half.shape[2], FF_CHUNK):
         cols = pl.ds(start, FF_CHUNK)
         d_hidden = lax.dot_general(cot_cur, w_out[layer_id, cols, :], NT, preferred_element_type=F32).astype(BF16)
         d_pre = (d_hidden.astype(F32) * acts_s[layer_id, rows, cols]).astype(BF16)
         d_pres.append(d_pre)
-        d_x += lax.dot_general(d_pre, w_in[layer_id, :, cols], NT, preferred_element_type=F32)
+        d_x += lax.dot_general(d_pre, w_half[layer_id, :, cols], NT, preferred_element_type=F32)
     cot[rows, :] = d_x.astype(BF16)
     cot_t = cot_cur.T
-    x_t = acts_x[layer_id, rows, :].T
-    for start, d_pre in zip(range(0, w_in.shape[2], FF_CHUNK), d_pres):
+    x_t = (acts_x[layer_id, rows, :].astype(F32) * 0.5).astype(BF16).T
+    for start, d_pre in zip(range(0, w_half.shape[2], FF_CHUNK), d_pres):
         cols = pl.ds(start, FF_CHUNK)
         sum_out_t[layer_id, :, cols] += jnp.dot(cot_t, acts_a[layer_id, rows, cols], preferred_element_type=F32)
         sum_in[layer_id, :, cols] += jnp.dot(x_t, d_pre, preferred_element_type=F32)
 
 
-def each_layer(layers, tokens, step):
-    part = tokens // PARTS
-
-    @pl.loop(0, layers // STRIDE)
-    def _(turn):
-        for pos in range(STRIDE):
-            for index in range(PARTS):
-                step(turn * STRIDE + pos, pl.ds(index * part, part))
+def each_layer(layers, tokens, parts, step):
+    part = tokens // parts
+    for layer_id in range(layers):
+        for index in range(parts):
+            step(layer_id, pl.ds(index * part, part))
 
 
 def mark_repeats(ids):
@@ -89,7 +90,7 @@
 
 def stage_kernel(stages, ids, d_out, stored_x, w_in, w_out, acc_in, acc_out, acc_emb,
                  marks, ids_own, ids_peer, tab_own, tab_peer, dx_all, gi_own, gi_recv, go_own, go_recv,
-                 acts_x, acts_a, acts_s, cot, dx_send, cot_in, sum_in, sum_out_t, acc_o, mark_buf, ids_mine, ids_buf,
+                 w_half, acts_x, acts_a, acts_s, cot, dx_send, cot_in, sum_in, sum_out_t, acc_o, mark_buf, ids_mine, ids_buf,
                  load_sem, ex_send, ex_recv, cot_send, cot_recv, bc_send, bc_recv, pr_send, pr_recv, loc_sem, g_sem, g_send, g_recv):
     stage = lax.axis_index('pp')
     rep = lax.axis_index('dp')
@@ -110,10 +111,11 @@
     load_emb = pltpu.make_async_copy(acc_emb, tab_own.at[pl.ds(0, vocab)], load_sem.at[2])
     load_emb.start()
     sum_out_t[...] = jnp.zeros_like(sum_out_t)
+    w_half[...] = (w_in[...].astype(F32) * 0.5).astype(BF16)
 
     def forward(step_id):
         acts_x[0] = stored_x[last - stage - step_id]
-        each_layer(layers, tokens, lambda layer_id, rows: forward_layer(layer_id, rows, w_in, w_out, acts_x, acts_a, acts_s))
+        each_layer(layers, tokens, FORWARD_PARTS, lambda layer_id, rows: forward_layer(layer_id, rows, layer_id == layers - 1, w_half, w_out, acts_x, acts_a, acts_s))
 
     micros, tokens = ids.shape
     for block in range(tokens // LANES):
@@ -125,12 +127,24 @@
         return pltpu.make_async_remote_copy(dx_send.at[step_id], cot_in.at[step_id], cot_send.at[step_id], cot_recv.at[step_id],
                                             device_id=(jnp.maximum(stage - 1, 0), rep), device_id_type=MESH)
 
-    def bc_copy(step_id, target):
-        return pltpu.make_async_remote_copy(dx_send.at[step_id], dx_all.at[rep, last - step_id], bc_send.at[target, step_id], bc_recv.at[step_id],
+    chunk_rows = d_out.shape[0] // CHUNKS
+
+    def piece(step_id, chunk):
+        return dx_all.at[rep, last - step_id, pl.ds(chunk * chunk_rows, chunk_rows)]
+
+    def sent(step_id, chunk):
+        return dx_send.at[step_id, pl.ds(chunk * chunk_rows, chunk_rows)]
+
+    def bc_copy(step_id, chunk, target):
+        return pltpu.make_async_remote_copy(sent(step_id, chunk), piece(step_id, chunk), bc_send.at[target, step_id, chunk], bc_recv.at[step_id, chunk],
                                             device_id=(target, rep), device_id_type=MESH)
 
-    def peer_copy(step_id, src):
-        return pltpu.make_async_remote_copy(src, dx_all.at[rep, last - step_id], pr_send.at[step_id], pr_recv.at[step_id],
+    def relay_copy(step_id, chunk):
+        return pltpu.make_async_remote_copy(piece(step_id, chunk), piece(step_id, chunk), bc_send.at[last, step_id, chunk], bc_recv.at[step_id, chunk],
+                                            device_id=(last, rep), device_id_type=MESH)
+
+    def peer_copy(step_id, chunk, src):
+        return pltpu.make_async_remote_copy(src, piece(step_id, chunk), pr_send.at[step_id, chunk], pr_recv.at[step_id, chunk],
                                             device_id=(stage, other), device_id_type=MESH)
 
     def local_copy(step_id):
@@ -156,7 +170,7 @@
                 cot_copy(step_id - 1).wait_recv()
                 cot[...] = cot_in[step_id - 1]
 
-            each_layer(layers, tokens, lambda back_id, rows: backward_layer(layers - 1 - back_id, rows, w_in, w_out, acts_x, acts_a, acts_s, cot, sum_in, sum_out_t))
+            each_layer(layers, tokens, BACKWARD_PARTS, lambda back_id, rows: backward_layer(layers - 1 - back_id, rows, w_half, w_out, acts_x, acts_a, acts_s, cot, sum_in, sum_out_t))
             dx_send[step_id] = cot[...]
 
             @pl.when(stage > 0)
@@ -165,9 +179,11 @@
 
             @pl.when(stage == 0)
             def _():
-                for target in range(1, stages):
-                    bc_copy(step_id, target).start()
-                peer_copy(step_id, dx_send.at[step_id]).start()
+                for first, second in zip(ROUTES[1], ROUTES[2]):
+                    bc_copy(step_id, first, 1).start()
+                    bc_copy(step_id, second, 2).start()
+                for chunk in range(CHUNKS):
+                    peer_copy(step_id, chunk, sent(step_id, chunk)).start()
                 local_copy(step_id).start()
 
     ex_ids.wait()
@@ -201,25 +217,33 @@
     for copy in keep + give:
         copy.start()
 
-    @pl.when(stage > 0)
-    def _():
-        for step_id in range(stages):
-            bc_copy(step_id, 0).wait_recv()
-            peer_copy(step_id, dx_all.at[rep, last - step_id]).start()
-        for step_id in range(stages):
-            @pl.when(stage + step_id <= last)
-            def _():
-                cot_copy(step_id).wait_send()
+    for place, order in ROUTES.items():
+        @pl.when(stage == place)
+        def _():
+            for step_id in range(stages):
+                for pos, chunk in enumerate(order):
+                    bc_copy(step_id, chunk, 0).wait_recv()
+                    if place < last and pos < CHUNKS // 2:
+                        relay_copy(step_id, chunk).start()
+                    peer_copy(step_id, chunk, piece(step_id, chunk)).start()
+            for step_id in range(stages):
+                if place < last:
+                    for chunk in order[:CHUNKS // 2]:
+                        relay_copy(step_id, chunk).wait_send()
+                if place + step_id <= last:
+                    cot_copy(step_id).wait_send()
 
     @pl.when(stage == 0)
     def _():
         for step_id in range(stages):
-            for target in range(1, stages):
-                bc_copy(step_id, target).wait_send()
+            for chunk in range(CHUNKS):
+                for target in (1, 2):
+                    bc_copy(step_id, chunk, target).wait_send()
             local_copy(step_id).wait()
 
     for step_id in range(stages):
-        peer_copy(step_id, dx_send.at[step_id]).wait()
+        for chunk in range(CHUNKS):
+            peer_copy(step_id, chunk, sent(step_id, chunk)).wait()
     for copy in keep + give:
         copy.wait()
     for copy in small:
@@ -296,12 +320,13 @@
             copy.start()
 
     half = emb_t.shape[0]
-    row_id = lax.broadcasted_iota(jnp.int32, (half, 2 * width), 0)
-    col_id = lax.broadcasted_iota(jnp.int32, (half, 2 * width), 1)
-    pick = jnp.where(lax.rem(col_id, width) == row_id + half * rep, 0.5, 0.0).astype(BF16)
+    row_id = lax.broadcasted_iota(jnp.int32, (half, width), 0)
+    col_id = lax.broadcasted_iota(jnp.int32, (half, width), 1)
+    pick = jnp.where(lax.rem(col_id, half) == row_id, 0.5, 0.0).astype(BF16)
+    mine = lax.broadcasted_iota(jnp.int32, (VOCAB_TILE, width), 1) // half == rep
     for start in range(0, emb_t.shape[1], VOCAB_TILE):
-        first = pl.multiple_of(step * emb_t.shape[1] + start, 8)
-        both = jnp.concatenate([rows_own[pl.ds(first, VOCAB_TILE), :].astype(BF16), rows_peer[pl.ds(first, VOCAB_TILE), :].astype(BF16)], axis=1)
+        rows = pl.ds(pl.multiple_of(step * emb_t.shape[1] + start, 8), VOCAB_TILE)
+        both = jnp.where(mine, rows_own[rows, :], pltpu.roll(rows_peer[rows, :], half, 1)).astype(BF16)
         emb_t[:, start:start + VOCAB_TILE] = lax.dot_general(pick, both, NT, preferred_element_type=F32)
 
     @pl.when(step == pl.num_programs(0) - 1)
@@ -342,6 +367,7 @@
                 jax.ShapeDtypeStruct((layers, half_o, hid), BF16),
             ],
             scratch_shapes=[
+                pltpu.VMEM((layers, hid, ff), BF16),
                 pltpu.VMEM((layers + 1, tokens, hid), BF16),
                 pltpu.VMEM((layers, tokens, ff), BF16),
                 pltpu.VMEM((layers, tokens, ff), F32),
@@ -356,11 +382,11 @@
                 pltpu.VMEM(lines.shape, jnp.int32),
                 dma((6,)), dma((2,)), dma((2,)),
                 dma((stages,)), dma((stages,)),
-                dma((stages, stages)), dma((stages,)),
-                dma((stages,)), dma((stages,)), dma((stages,)),
+                dma((stages, stages, CHUNKS)), dma((stages, CHUNKS)),
+                dma((stages, CHUNKS)), dma((stages, CHUNKS)), dma((stages,)),
                 dma((2,)), dma((2,)), dma((2,)),
             ],
-            compiler_params=pltpu.CompilerParams(collective_id=0, has_side_effects=True, vmem_limit_bytes=28 * 2**20),
+            compiler_params=pltpu.CompilerParams(collective_id=0, has_side_effects=True, vmem_limit_bytes=30 * 2**20),
         )(tok_ids, d_out[0], stored_x[0], w_in, w_out, acc_in[:, 0], acc_out[:, 0], emb_rows)
 
         resident = lambda x: pltpu.with_memory_space_constraint(x, pltpu.VMEM)
@@ -384,7 +410,7 @@
                 pltpu.VMEM((layers, half_o, hid), F32),
                 dma((6,)),
             ],
-            compiler_params=pltpu.CompilerParams(vmem_limit_bytes=28 * 2**20),
+            compiler_params=pltpu.CompilerParams(vmem_limit_bytes=30 * 2**20),
         )(ids_own, ids_peer, marks, resident(tab_own), resident(tab_peer), resident(dx_all), gi_own, gi_recv, go_own, go_recv)
         return grad_in, grad_out, emb_t.T
 

time: 64.6 us -> 61.9 us (0.958)
  Pallas kernels: 63.8 us -> 61.5 us
    pallas_call x1, Pallas kernels: 47.5 us -> 46.1 us  [device_body(): pl.pallas_call(functools.partial(stage_kernel, stages), name='stage_pipel...]
    pallas_call x1, Pallas kernels: 16.3 us -> 15.4 us  [device_body(): pl.pallas_call(finish_kernel, name='finish', grid=(pl.cdiv(vocab, VOCAB_B...]
where the time goes in v4:
time: 61.9 us; the launch traced here: 62.1 us
  Pallas kernels  61.5 us (99%)
  between operations  0.64 us (1%)
    pallas_call x1, Pallas kernels, device_body(): pl.pallas_call(functools.partial(stage_kernel, stages), name='stage_pipel...  46.1 us
    pallas_call x1, Pallas kernels, device_body(): pl.pallas_call(finish_kernel, name='finish', grid=(pl.cdiv(vocab, VOCAB_B...  15.4 us

profile of v4, /device:TPU:7, one launch (start us, length us, event | category | flops | bytes accessed | tf_op | source)
XLA Modules:
  0.0 62.1 jit_solution(2935130546286313232)
XLA Ops:
  0.6 46.1 %stage_pipeline.1 = (s32[16,128]{1,0:T(8,128)}, s32[16,128]{1,0:T(8,128)}, s32[16,128]{1,0:T(8,128)}, f32[30720,1,128]{2,1,0:T(1,128)S(1)}, f32[30720,1,128]{2,1...) custom-call(s32[4,512]{1,0:T(4,128)} %ids.1, ...), custom_call_target="tpu_custom_call" | custom-call | tf_op jit(solution)/shard_map/stage_pipeline/pallas_call | solution.py:352
  46.8 15.4 %finish.1 = (f32[64,30522]{1,0:T(8,128)}, f32[8,64,512]{2,1,0:T(8,128)}, f32[8,256,128]{2,1,0:T(8,128)}) custom-call(s32[16,128]{1,0:T(8,128)} %get-tuple-element.16.ids_own, s32[16,128]{1,0:T(8,128)} %get-tuple-element.17.ids_peer, s32[16,128]{1,0:T(8,128)} %get-tuple-element.18.marks, f32[30720,1,128]{2,1,0:T(1,128)S(1)} %get-tuple-element.19.tab_own, ...), custom_call_target="tpu_custom_call" | custom-call | tf_op jit(solution)/shard_map/finish/pallas_call | solution.py:394

commit v5 on v4

--- a/solution.py
+++ b/solution.py
@@ -17,7 +17,7 @@
 FORWARD_PARTS = 2
 BACKWARD_PARTS = 1
 GROUP = 32
-BATCH = 2
+BATCH = 4
 LANES = 128
 CHUNKS = 4
 ROUTES = {1: (0, 1, 2, 3), 2: (2, 3, 0, 1), 3: (0, 2, 1, 3)}
@@ -278,9 +278,7 @@
             micro = lax.rem(line, micros)
             token = (line // micros) * LANES
 
-            @pl.loop(0, LANES // GROUP)
-            def _(group):
-                base = pl.multiple_of(group * GROUP, GROUP)
+            for base in range(0, LANES, GROUP):
                 repeated = marks[line, base] != 0
 
                 @pl.when(repeated)

time: 61.9 us -> 59.5 us (0.961); the launches traced: 62.1 us -> 58.7 us
  Pallas kernels: 61.5 us -> 58.1 us
    pallas_call x1, Pallas kernels: 15.4 us -> 12 us  [device_body(): pl.pallas_call(finish_kernel, name='finish', grid=(pl.cdiv(vocab, VOCAB_B...]
where the time goes in v5:
time: 59.5 us; the launch traced here: 58.7 us
  Pallas kernels  58.1 us (98%)
  between operations  0.64 us (1%)
    pallas_call x1, Pallas kernels, device_body(): pl.pallas_call(functools.partial(stage_kernel, stages), name='stage_pipel...  46.1 us
    pallas_call x1, Pallas kernels, device_body(): pl.pallas_call(finish_kernel, name='finish', grid=(pl.cdiv(vocab, VOCAB_B...  12 us

profile of v5, /device:TPU:7, one launch (start us, length us, event | category | flops | bytes accessed | tf_op | source)
XLA Modules:
  0.0 58.7 jit_solution(15538500875389059420)
XLA Ops:
  0.6 46.1 %stage_pipeline.1 = (s32[16,128]{1,0:T(8,128)}, s32[16,128]{1,0:T(8,128)}, s32[16,128]{1,0:T(8,128)}, f32[30720,1,128]{2,1,0:T(1,128)S(1)}, f32[30720,1,128]{2,1...) custom-call(s32[4,512]{1,0:T(4,128)} %ids.1, ...), custom_call_target="tpu_custom_call" | custom-call | tf_op jit(solution)/shard_map/stage_pipeline/pallas_call | solution.py:350
  46.8 12.0 %finish.1 = (f32[64,30522]{1,0:T(8,128)}, f32[8,64,512]{2,1,0:T(8,128)}, f32[8,256,128]{2,1,0:T(8,128)}) custom-call(s32[16,128]{1,0:T(8,128)} %get-tuple-element.16.ids_own, s32[16,128]{1,0:T(8,128)} %get-tuple-element.17.ids_peer, s32[16,128]{1,0:T(8,128)} %get-tuple-element.18.marks, f32[30720,1,128]{2,1,0:T(1,128)S(1)} %get-tuple-element.19.tab_own, ...), custom_call_target="tpu_custom_call" | custom-call | tf_op jit(solution)/shard_map/finish/pallas_call | solution.py:392
